TPU v7x, 512 devices: a whole 4x8x8 slice. The times are simulated.
512 devices in a mesh: win: 128 (over z, y, core), tile: 4 (over x).
Axes of the slice: x: 4, y: 8, z: 8, core: 2. Of those that a mesh axis runs over, the one named last changes fastest.
Arguments:
- right_side: float32 [128, 2, 128, 1024], P('win', None, 'tile'), may hold values from -64 to 64
- error_weight: float32 [128, 2, 128, 1024], P('win', None, 'tile'), may hold values from 0.5 to 4
- coeffs: float32 [4, 128, 2, 128, 1024], P(None, 'win', None, 'tile'), may hold values from 0.1 to 0.4
- obs_block: int32 [128, 128], P('win', 'tile'), may hold values from 0 to 511
- obs_pos: int32 [128, 128, 128], P('win', 'tile'), may hold values from 0 to 127
- obs_weight: float32 [128, 128, 128], P('win', 'tile'), may hold values from 0.5 to 4
Outputs:
- solution_field: float32 [128, 2, 128, 1024], P('win', None, 'tile')
- residual: float32 [128, 2, 128, 1024], P('win', None, 'tile')
All inputs are finite; a program needn't handle non-finite values.
Results may differ from a plain program's by a relative error of at most 0.0001.
Values sent between devices are 32-bit elements; how exact they have to be, the bound alone decides.
No kernel may reach another device: no remote copies, remote signals or barrier semaphores. Data moves between devices by JAX's collectives and lax.ppermute only.
A program may use at most 64 MiB of HBM per device.

v0:
```python
import jax
import jax.numpy as jnp
from jax import lax
from jax.experimental import pallas as pl
from jax.experimental.pallas import tpu as pltpu
from jax.sharding import Mesh
from jax.sharding import PartitionSpec as P


WIN = ("win_0", "win_1", "win_2")
THETA = 6.0
G = 8
F32 = jnp.float32


def call(body, out_shape, aliases=None, hbm=False, count=0, scratch=()):
    place = pltpu.HBM if hbm else pltpu.VMEM
    return pl.pallas_call(
        body,
        out_shape=out_shape,
        in_specs=[pl.BlockSpec(memory_space=place) for _ in range(count)],
        out_specs=[pl.BlockSpec(memory_space=pltpu.VMEM) for _ in out_shape],
        scratch_shapes=scratch,
        input_output_aliases=aliases or {},
        compiler_params=pltpu.CompilerParams(vmem_limit_bytes=24 * 2**20),
    )


def in_hbm(x):
    return pltpu.with_memory_space_constraint(x, pltpu.HBM)


def shape(*dims):
    return jax.ShapeDtypeStruct(dims, F32)


def west(x):
    return pltpu.roll(x, 1, axis=1)


def east(x):
    return pltpu.roll(x, x.shape[1] - 1, axis=1)


def north_of(ref, lev, tile):
    if tile == 0:
        return pltpu.roll(ref[lev, 0:8, :], 1, axis=0)
    return ref[lev, 8 * tile - 1 : 8 * tile + 7, :]


def south_of(ref, lev, tile, tiles):
    if tile == tiles - 1:
        return pltpu.roll(ref[lev, 8 * tile : 8 * tile + 8, :], 7, axis=0)
    return ref[lev, 8 * tile + 1 : 8 * tile + 9, :]


def folded(x):
    total = x[:, 0:128]
    for at in range(128, x.shape[1], 128):
        total = total + x[:, at : at + 128]
    return total


PARTS = (("b", 0, 5), ("c", 0, 4), ("c", 1, 5), ("c", 2, 4), ("c", 3, 4), ("w", 0, 5), ("d", 0, 4), ("p", 0, 1))
PER_LEVEL = sum(count for _, _, count in PARTS)
EDGES = 20


def ghost_items(levels):
    at = 0
    for lev in range(levels):
        for name, f, rows in PARTS:
            yield name, f, lev, at, rows
            at += rows


def pack_kernel(
    b_hbm, c_hbm, w_hbm, pos_hbm, block_hbm, weight_hbm,
    north, south, b_e, c_e, w_e, d_e,
    pos, block, weight, blocks, sems,
):
    levels, rows, width = b_hbm.shape
    per_row = width // 128
    own = pl.ds(G, rows)
    pairs = (
        (pos_hbm, pos),
        (weight_hbm, weight),
        (block_hbm, block),
        (b_hbm, b_e.at[:, own, :]),
        (w_hbm, w_e.at[:, own, :]),
        (c_hbm, c_e.at[:, :, own, :]),
    )
    moves = [pltpu.make_async_copy(src, dst, sems.at[i]) for i, (src, dst) in enumerate(pairs)]
    for move in moves:
        move.start()
    blank = jnp.zeros((G, width), F32)
    for lev in range(levels):
        for out in (b_e.at[lev], w_e.at[lev], d_e.at[lev], *(c_e.at[f, lev] for f in range(4))):
            out[0:G, :] = blank
            out[G + rows :, :] = blank
    blocks[...] = jnp.zeros(blocks.shape, F32)
    for move in moves[:3]:
        move.wait()
    hot = block_sums(pos[...].astype(F32), weight[...])
    for i in range(hot.shape[0]):
        at = pl.ds(block[0, i], 1)
        blocks[at, :] = blocks[at, :] + hot[i : i + 1, :]
    for lev in range(levels):
        for j in range(per_row):
            first = lev * rows * per_row + j
            d_e[lev, G : G + rows, j * 128 : j * 128 + 128] = blocks[
                pl.ds(first, rows, stride=per_row), :
            ]
    for move in moves[3:]:
        move.wait()
    for name, f, lev, at, count in ghost_items(levels):
        for out, first in ((north, G), (south, G + rows - count)):
            if name == "p":
                tile = 1 if out is north else rows // 8
                image = model_tile(b_e, c_e, lev, tile, 2 + rows // 8)
                piece = image[4:5, :] if out is north else image[3:4, :]
            else:
                src = {"b": b_e, "c": c_e.at[f], "w": w_e, "d": d_e}[name]
                piece = src[lev, first : first + count, :]
            out[at : at + count, :] = piece


def block_sums(pos, weight):
    n, width = pos.shape
    groups = width // n

    def packed(x):
        turned = x.T
        return jnp.concatenate([turned[g * n : g * n + n, :] for g in range(groups)], axis=1)

    pos, weight = packed(pos), packed(weight)
    cell = lax.broadcasted_iota(jnp.int32, (width, width), 0).astype(F32)
    total = jnp.zeros((width, width), F32)
    for i in range(n):
        here = jnp.broadcast_to(pos[i : i + 1, :], (width, width))
        value = jnp.broadcast_to(weight[i : i + 1, :], (width, width))
        total = total + jnp.where(here == cell, value, 0.0)
    shift = width // 2
    while shift >= n:
        total = total + pltpu.roll(total, shift, axis=1)
        shift //= 2
    return total.T[0:n, :]


def extend_kernel(b_e, c_e, w_e, cross):
    levels, total, _ = b_e.shape
    rows = total - 2 * G
    for lev in range(levels):
        cross[levels + lev, :, :] = w_e[lev, G : G + rows, :]

    @pl.when(core_is_one())
    def _():
        for lev in range(levels):
            for tile in range(1, 1 + rows // 8):
                at = 8 * tile - G
                cross[lev, at : at + 8, :] = model_tile(b_e, c_e, lev, tile, 2 + rows // 8)

    @pl.when(jnp.logical_not(core_is_one()))
    def _():
        for lev in range(levels):
            cross[lev, :, :] = b_e[lev, G : G + rows, :]


def model_tile(q, c, lev, tile, tiles):
    here = q[lev, 8 * tile : 8 * tile + 8, :]
    at = slice(8 * tile, 8 * tile + 8)
    return (
        c[0, lev, at, :] * here
        + c[1, lev, at, :] * (north_of(q, lev, tile) + south_of(q, lev, tile, tiles))
        + c[2, lev, at, :] * east(here)
        + c[3, lev, at, :] * west(here)
    )


def propagate(q, c, p):
    levels, rows, _ = q.shape
    for lev in range(levels):
        for tile in range(rows // 8):
            p[lev, 8 * tile : 8 * tile + 8, :] = model_tile(q, c, lev, tile, rows // 8)


def post(out, values, lev):
    reach = out.shape[1] - (values.shape[1] - 2 * G)
    first = G - reach // 2
    out[lev, :, :] = values[lev, first : first + out.shape[1], :]


def core_is_one():
    return lax.axis_index("win_2") == 1


def ghosts_kernel(from_north, from_south, b_in, c_in, w_in, d_in, b_e, c_e, w_e, d_e, p, cross, within):
    levels, total, width = b_e.shape
    rows = total - 2 * G

    def fill(names):
        for name, f, lev, at, count in ghost_items(levels):
            if name in names:
                out = {"b": b_e, "c": c_e.at[f], "w": w_e, "d": d_e, "p": p}[name]
                reach = 5 if name == "p" else count
                low, high = G - reach, G + rows + reach - count
                out[lev, low : low + count, :] = from_north[at : at + count, :]
                out[lev, high : high + count, :] = from_south[at : at + count, :]

    fill("bcwd")
    propagate(b_e, c_e, p)
    fill("p")

    @pl.when(core_is_one())
    def _():
        for lev in range(levels):
            at = lev * EDGES
            cross[at : at + 5, :] = p[lev, 4:9, :]
            cross[at + 5 : at + 10, :] = p[lev, G + rows - 1 : G + rows + 4, :]
            cross[at + 10 : at + EDGES, :] = jnp.zeros((EDGES - 10, width), F32)
            within[lev] = b_e[lev]
            within[levels + lev] = w_e[lev]

    @pl.when(jnp.logical_not(core_is_one()))
    def _():
        for lev in range(levels):
            for f, field in enumerate((b_e, w_e)):
                low, high = lev * EDGES + 10 * f, lev * EDGES + 10 * f + 5
                cross[low : low + 5, :] = field[lev, 3:8, :]
                cross[high : high + 5, :] = field[lev, G + rows : G + rows + 5, :]
            within[lev] = p[lev]
            within[levels + lev] = p[lev]


def unposted(ref, lev, tile, tiles):
    if tile == 0:
        return pltpu.roll(ref[lev, 0:8, :], 4, axis=0)
    if tile == tiles - 1:
        return pltpu.roll(ref[lev, 8 * tile - 8 : 8 * tile, :], 4, axis=0)
    return ref[lev, 8 * tile - 4 : 8 * tile + 4, :]


def second_half(q, c, w, d, p, v_next, w_next, p_prev, out, edge):
    levels, total, _ = q.shape
    tiles = total // 8
    for lev in range(levels):
        for tile in range(tiles):
            at = slice(8 * tile, 8 * tile + 8)
            here, weight = q[lev, at, :], w[lev, at, :]
            following = w_next(lev, tile) * (v_next(lev, tile) - p[lev, at, :])
            edge[lev, at, :] = c[1, lev, at, :] * following
            out[lev, at, :] = (
                (weight + d[lev, at, :] - THETA) * here
                - weight * p_prev(lev, tile)
                - c[0, lev, at, :] * following
                - west(c[2, lev, at, :] * following)
                - east(c[3, lev, at, :] * following)
            )
    for lev in range(levels):
        for tile in range(tiles):
            at = slice(8 * tile, 8 * tile + 8)
            value = out[lev, at, :] - (north_of(edge, lev, tile) + south_of(edge, lev, tile, tiles))
            if tile in (0, tiles - 1):
                value = jnp.where(w[lev, at, :] > 0.0, value, 0.0)
            out[lev, at, :] = value


def products_kernel(x, y, out):
    levels, total, _ = x.shape
    totals = [jnp.zeros((8, 128), F32) for _ in range(out.shape[0])]
    for lev in range(levels):
        for at in range(G, total - G, 8):
            u, v = x[lev, at : at + 8, :], y[lev, at : at + 8, :]
            for i, (a, b) in enumerate(((u, v), (v, v), (u, u))[: len(totals)]):
                totals[i] = totals[i] + folded(a * b)
    for i, part in enumerate(totals):
        out[i] = part


def send_both(q, p, cross, within):
    def send(forward, backward):
        for lev in range(q.shape[0]):
            post(forward, p, lev)
            post(backward, q, lev)

    @pl.when(core_is_one())
    def _():
        send(cross, within)

    @pl.when(jnp.logical_not(core_is_one()))
    def _():
        send(within, cross)


def first_apply_kernel(
    b_e, c, w, d, p0, cross_own, cross_in, within_in,
    q1, p1, w_next, cross, within, edge, v_next, p_prev,
):
    levels, total, width = b_e.shape
    rows = total - 2 * G
    blank = jnp.zeros((G, width), F32)

    @pl.when(core_is_one())
    def _():
        for lev in range(levels):
            p_prev[lev] = within_in[lev]
            for f, out in enumerate((v_next, w_next)):
                low, high = lev * EDGES + 10 * f, lev * EDGES + 10 * f + 5
                out[lev, 0:G, :] = blank
                out[lev, G : G + rows, :] = cross_own[f * levels + lev]
                out[lev, G + rows :, :] = blank
                out[lev, 3:8, :] = cross_in[low : low + 5, :]
                out[lev, G + rows : G + rows + 5, :] = cross_in[high : high + 5, :]

    @pl.when(jnp.logical_not(core_is_one()))
    def _():
        for lev in range(levels):
            at = lev * EDGES
            v_next[lev] = within_in[lev]
            w_next[lev] = within_in[levels + lev]
            p_prev[lev, 0:G, :] = blank
            p_prev[lev, G : G + rows, :] = cross_own[lev]
            p_prev[lev, G + rows :, :] = blank
            p_prev[lev, 4:9, :] = cross_in[at : at + 5, :]
            p_prev[lev, G + rows - 1 : G + rows + 4, :] = cross_in[at + 5 : at + 10, :]

    def tile_of(ref):
        return lambda lev, tile: ref[lev, 8 * tile : 8 * tile + 8, :]

    second_half(
        b_e, c, w, d, p0, tile_of(v_next), tile_of(w_next), tile_of(p_prev), q1, edge
    )
    propagate(q1, c, p1)
    send_both(q1, p1, cross, within)


def apply_kernel(
    q1, c, w, d, p1, w_next, cross_in, within_in, q2, p2, cross, within, edge
):
    _, total, _ = q1.shape
    tiles = total // 8
    one = core_is_one()

    def v_next(lev, tile):
        return jnp.where(
            one, unposted(cross_in, lev, tile, tiles), unposted(within_in, lev, tile, tiles)
        )

    def p_prev(lev, tile):
        return jnp.where(
            one, unposted(within_in, lev, tile, tiles), unposted(cross_in, lev, tile, tiles)
        )

    second_half(
        q1, c, w, d, p1, v_next,
        lambda lev, tile: w_next[lev, 8 * tile : 8 * tile + 8, :], p_prev, q2, edge,
    )
    propagate(q2, c, p2)
    send_both(q2, p2, cross, within)


def moments_kernel(q2, c, w, d, p2, w_next, cross_in, within_in, sums_1, sums_2, out, q3, edge, v_next, p_prev):
    levels, total, _ = q2.shape
    tiles = total // 8
    one = core_is_one()
    first = jnp.logical_and(
        lax.axis_index("win_0") + lax.axis_index("win_1") == 0, jnp.logical_not(one)
    )

    @pl.when(one)
    def _():
        v_next[...] = cross_in[...]
        p_prev[...] = within_in[...]

    @pl.when(jnp.logical_not(one))
    def _():
        v_next[...] = within_in[...]
        p_prev[...] = cross_in[...]

    last = jnp.zeros((8, 128), F32)
    for lev in range(levels):
        for tile in range(1, tiles - 1):
            at = slice(8 * tile, 8 * tile + 8)
            here, weight = q2[lev, at, :], w[lev, at, :]
            gap = v_next[lev, 8 * tile - 4 : 8 * tile + 4, :] - p2[lev, at, :]
            following = w_next[lev, at, :] * gap
            diagonal = d[lev, at, :] - THETA
            own = diagonal + jnp.where(first, weight, 0.0)
            last = last + folded(following * gap + own * here * here)
            edge[lev, at, :] = c[1, lev, at, :] * following
            q3[lev, at, :] = (
                (weight + diagonal) * here
                - weight * p_prev[lev, 8 * tile - 4 : 8 * tile + 4, :]
                - c[0, lev, at, :] * following
                - west(c[2, lev, at, :] * following)
                - east(c[3, lev, at, :] * following)
            )
        for row, at in ((G - 1, 3), (total - G, total - G - 4)):
            following = w_next[lev, row : row + 1, :] * (
                v_next[lev, at : at + 1, :] - p2[lev, row : row + 1, :]
            )
            edge[lev, row : row + 1, :] = c[1, lev, row : row + 1, :] * following
        for tile in range(1, tiles - 1):
            at = slice(8 * tile, 8 * tile + 8)
            q3[lev, at, :] = q3[lev, at, :] - (
                north_of(edge, lev, tile) + south_of(edge, lev, tile, tiles)
            )
    lane = lax.broadcasted_iota(jnp.int32, (1, 128), 1)
    result = jnp.zeros((1, 128), F32)
    parts = [sums_1[2], sums_1[0], sums_1[1], sums_2[0], sums_2[1], last]
    for i, part in enumerate(parts):
        total_i = jnp.sum(jnp.sum(part, axis=0, keepdims=True), axis=1, keepdims=True)
        result = jnp.where(lane == i, jnp.broadcast_to(total_i, (1, 128)), result)
    for i in range(out.shape[0]):
        out[i] = result


def spread_kernel(x, out):
    total = summed(x)
    for i in range(out.shape[0]):
        out[i] = total


def summed(x):
    parts = [x[i] for i in range(x.shape[0])]
    while len(parts) > 1:
        parts = [a + b for a, b in zip(parts[::2], parts[1::2])]
    return parts[0]


def times_a(v):
    longer = [THETA * x for x in v] + [0.0]
    return [longer[i] + (v[i - 1] if i else 0.0) for i in range(len(longer))]


def inner(u, v, mu):
    return sum(x * y * mu[i + j] for i, x in enumerate(u) for j, y in enumerate(v))


def plus(u, scale, v):
    size = max(len(u), len(v))
    u, v = u + [0.0] * (size - len(u)), v + [0.0] * (size - len(v))
    return [x + scale * y for x, y in zip(u, v)]


def coordinates(mu, iters=3):
    x, r, p = [0.0], [1.0], [1.0]
    rr = mu[0]
    for i in range(iters):
        image = times_a(p)
        alpha = rr / inner(p, image, mu)
        x = plus(x, alpha, p)
        r = plus(r, -alpha, image)
        if i + 1 < iters:
            new = inner(r, r, mu)
            p = plus(r, new / rr, p)
            rr = new
    return x, r


def finish_kernel(parts, q0, q1, q2, q3, solution_field, residual):
    levels, rows, width = solution_field.shape
    total = summed(parts)
    mu = [jnp.broadcast_to(total[:, i : i + 1], (8, 128)) for i in range(6)]
    x, r = coordinates(mu)
    wide = lambda v: jnp.concatenate([v] * (width // 128), axis=1)
    x = [wide(v) for v in x]
    r = [wide(v) for v in r]
    for lev in range(levels):
        for at in range(0, rows, 8):
            s = [q[lev, G + at : G + at + 8, :] for q in (q0, q1, q2, q3)]
            solution_field[lev, at : at + 8, :] = x[0] * s[0] + x[1] * s[1] + x[2] * s[2]
            residual[lev, at : at + 8, :] = r[0] * s[0] + r[1] * s[1] + r[2] * s[2] + r[3] * s[3]


def shifted(x, axis, by):
    count = lax.axis_size(axis)
    return lax.ppermute(x, axis, [(i, i + by) for i in range(count) if 0 <= i + by < count])


def exchanged(cross, within):
    cross = over_chips(cross)
    within = on_chip(within)
    return cross, within


def over_chips(x):
    count = lax.axis_size(WIN)
    pairs = [(i, i + 1) for i in range(1, count - 1, 2)]
    return lax.ppermute(x, WIN, pairs + [(b, a) for a, b in pairs])


def on_chip(x):
    return lax.ppermute(x, "win_2", [(0, 1), (1, 0)])


def solve(right_side, error_weight, coeffs, obs_block, obs_pos, obs_weight):
    b, w, c = right_side[0], error_weight[0], coeffs[:, 0]
    levels, rows, width = b.shape
    total = rows + 2 * G
    field = shape(levels, total, width)
    fields = shape(4, levels, total, width)
    own = shape(levels, rows, width)
    ghost = shape(levels * PER_LEVEL, width)
    edges = shape(levels * EDGES, width)
    message = shape(levels, rows + 8, width)
    scratch = pltpu.VMEM((levels, total, width), F32)

    north, south, b_e, c_e, w_e, d_e = call(
        pack_kernel,
        [ghost, ghost, field, fields, field, field],
        hbm=True,
        count=6,
        scratch=(
            pltpu.VMEM(obs_pos.shape[1:], jnp.int32),
            pltpu.SMEM(obs_block.shape, jnp.int32),
            pltpu.VMEM(obs_weight.shape[1:], F32),
            pltpu.VMEM((b.size // 128, 128), F32),
            pltpu.SemaphoreType.DMA((6,)),
        ),
    )(*(in_hbm(x) for x in (b, c, w, obs_pos[0], obs_block, obs_weight[0])))
    from_south = shifted(north, "tile", -1)
    from_north = shifted(south, "tile", 1)
    (cross_own,) = call(extend_kernel, [shape(2 * levels, rows, width)], count=3)(b_e, c_e, w_e)
    cross_own = over_chips(cross_own)
    b_e, c_e, w_e, d_e, p0, cross, within = call(
        ghosts_kernel,
        [field, fields, field, field, field, edges, shape(2 * levels, total, width)],
        aliases={2: 0, 3: 1, 4: 2, 5: 3},
        count=6,
    )(from_north, from_south, b_e, c_e, w_e, d_e)
    cross, within = exchanged(cross, within)
    q1, p1, w_next, cross, within = call(
        first_apply_kernel,
        [field, field, field, message, message],
        count=8,
        scratch=(scratch,) * 3,
    )(b_e, c_e, w_e, d_e, p0, cross_own, cross, within)
    cross, within = exchanged(cross, within)
    (sums_1,) = call(products_kernel, [shape(3, 8, 128)], count=2)(b_e, q1)
    q2, p2, cross, within = call(
        apply_kernel, [field, field, message, message], count=8, scratch=(scratch,)
    )(q1, c_e, w_e, d_e, p1, w_next, cross, within)
    cross, within = exchanged(cross, within)
    (sums_2,) = call(products_kernel, [shape(2, 8, 128)], count=2)(q1, q2)
    near, far = ("win_0", "win_2"), ("win_1", "tile")
    moments, q3 = call(
        moments_kernel,
        [shape(lax.axis_size(near), 1, 128), field],
        count=10,
        scratch=(scratch,) + (pltpu.VMEM((levels, rows + 8, width), F32),) * 2,
    )(q2, c_e, w_e, d_e, p2, w_next, cross, within, sums_1, sums_2)
    moments = lax.all_to_all(moments, near, 0, 0, tiled=True)
    (moments,) = call(spread_kernel, [shape(lax.axis_size(far), 1, 128)], count=1)(moments)
    moments = lax.all_to_all(moments, far, 0, 0, tiled=True)
    solution_field, residual = call(finish_kernel, [own, own], count=5)(moments, b_e, q1, q2, q3)
    return solution_field[None], residual[None]


def solution(mesh):
    split = Mesh(
        mesh.devices.reshape(8, 8, 2, mesh.shape["tile"]), ("win_0", "win_1", "win_2", "tile")
    )
    in_specs = (
        P(WIN, None, "tile", None),
        P(WIN, None, "tile", None),
        P(None, WIN, None, "tile", None),
        P(WIN, "tile"),
        P(WIN, "tile", None),
        P(WIN, "tile", None),
    )
    out_specs = (P(WIN, None, "tile", None), P(WIN, None, "tile", None))
    return jax.shard_map(solve, mesh=split, in_specs=in_specs, out_specs=out_specs, check_vma=False)
```

profile of v0, /device:TPU:1, one launch (start us, length us, event | category | flops | bytes accessed | tf_op | source)
XLA Modules:
  0.0 91.1 jit_solution(3327470558805252414)
XLA Ops:
  0.6 1.8 %shard_map.77 = (f32[64,1024]{1,0:T(8,128)S(1)}, f32[64,1024]{1,0:T(8,128)S(1)}, f32[2,48,1024]{2,1,0:T(8,128)S(1)}, f32[4,2,48,1024]{3,2,1,0:T(8,128)S(1)}, f32...) custom-call(f32[2,32,1024]{2,1,0:T(8,128)} %bitcast.8, f32[4,2,32,1024]{3,2,1,0:T(8,128)} %bitcast.7, ...), custom_call_target="tpu_custom_call" | custom-call | tf_op jit(solution)/shard_map/pallas_call | solution.py:509
  2.5 3.9 %collective-permute-start = (f32[64,1024]{1,0:T(8,128)S(1)}, f32[64,1024]{1,0:T(8,128)S(1)}, u32[]{:S(2)}, u32[]{:S(2)}) collective-permute-start(f32[64,1024]{1,0:T(8,128)S(1)} %get-tuple-element.28), channel_id=1, source_target_pairs={{0,1},{1,2},{2,3},{4,5},{5,6},{6,7},{8,9},{9,10},{10,11},{12,13},{... | collective-permute-start | bytes 786440 | tf_op jit(solution)/shard_map/ppermute | solution.py:478
  6.4 1.3 %collective-permute-start.1 = (f32[64,1024]{1,0:T(8,128)S(1)}, f32[64,1024]{1,0:T(8,128)S(1)}, u32[]{:S(2)}, u32[]{:S(2)}) collective-permute-start(f32[64,1024]{1,0:T(8,128)S(1)} %get-tuple-element.29), channel_id=1, source_target_pairs={{1,0},{2,1},{3,2},{5,4},{6,5},{7,6},{9,8},{10,9},{11,10},{13,12},{... | collective-permute-start | bytes 786440 | tf_op jit(solution)/shard_map/ppermute | solution.py:478
  7.7 0.2 shard_map.79
  7.9 1.8 %collective-permute-done.from_north = f32[64,1024]{1,0:T(8,128)S(1)} collective-permute-done((f32[64,1024]{1,0:T(8,128)S(1)}, f32[64,1024]{1,0:T(8,128)S(1)}, u32[]{:S(2)}, u32[]{:S(2)}) %collective-permute-start) | collective-permute-done | bytes 262176 | tf_op jit(solution)/shard_map/ppermute | solution.py:478
  9.7 3.8 %collective-permute-done.1.from_south = f32[64,1024]{1,0:T(8,128)S(1)} collective-permute-done((f32[64,1024]{1,0:T(8,128)S(1)}, f32[64,1024]{1,0:T(8,128)S(1)}, u32[]{:S(2)}, u32[]{:S(2)}) %collective-permute-start.1) | collective-permute-done | bytes 262176 | tf_op jit(solution)/shard_map/ppermute | solution.py:478
  13.5 0.4 shard_map.78
  13.9 7.2 %collective-permute-start.4 = (f32[4,48,1024]{2,1,0:T(8,128)S(1)}, f32[4,48,1024]{2,1,0:T(8,128)S(1)}, u32[]{:S(2)}, u32[]{:S(2)}) collective-permute-start(f32[4,48,1024]{2,1,0:T(8,128)S(1)} %get-tuple-element.40), channel_id=1, source_target_pairs={{0,4},{4,0},{1,5},{5,1},{2,6},{6,2},{3,7},{7,3},{8,12},{12,8},{9,1... | collective-permute-start | bytes 2359304 | tf_op jit(solution)/shard_map/ppermute | solution.py:494
  21.2 1.9 %collective-permute-start.2 = (f32[4,32,1024]{2,1,0:T(8,128)S(1)}, f32[4,32,1024]{2,1,0:T(8,128)S(1)}, u32[]{:S(2)}, u32[]{:S(2)}) collective-permute-start(f32[4,32,1024]{2,1,0:T(8,128)S(1)} %shard_map.79), channel_id=1, source_target_pairs={{4,8},{12,16},{20,24},{28,32},{36,40},{44,48},{52,56},{60,64},{68,... | collective-permute-start | bytes 1572872 | tf_op jit(solution)/shard_map/ppermute | solution.py:490
  23.1 3.6 %collective-permute-start.3 = (f32[40,1024]{1,0:T(8,128)S(1)}, f32[40,1024]{1,0:T(8,128)S(1)}, u32[]{:S(2)}, u32[]{:S(2)}) collective-permute-start(f32[40,1024]{1,0:T(8,128)S(1)} %get-tuple-element.39), channel_id=1, source_target_pairs={{4,8},{12,16},{20,24},{28,32},{36,40},{44,48},{52,56},{60,64},{68,... | collective-permute-start | bytes 491528 | tf_op jit(solution)/shard_map/ppermute | solution.py:490
  26.8 6.7 %collective-permute-done.3.cross_in = f32[40,1024]{1,0:T(8,128)S(1)} collective-permute-done((f32[40,1024]{1,0:T(8,128)S(1)}, f32[40,1024]{1,0:T(8,128)S(1)}, u32[]{:S(2)}, u32[]{:S(2)}) %collective-permute-start.3) | collective-permute-done | bytes 163872 | tf_op jit(solution)/shard_map/ppermute | solution.py:490
  33.4 0.0 collective-permute-done.2.cross_own
  33.4 0.0 collective-permute-done.4.within_in
  33.5 0.7 shard_map.80
  34.2 1.9 %collective-permute-start.5 = (f32[2,40,1024]{2,1,0:T(8,128)S(1)}, f32[2,40,1024]{2,1,0:T(8,128)S(1)}, u32[]{:S(2)}, u32[]{:S(2)}) collective-permute-start(f32[2,40,1024]{2,1,0:T(8,128)S(1)} %get-tuple-element.44), channel_id=1, source_target_pairs={{4,8},{12,16},{20,24},{28,32},{36,40},{44,48},{52,56},{60,64},{68,... | collective-permute-start | bytes 983048 | tf_op jit(solution)/shard_map/ppermute | solution.py:490
  36.1 1.9 %collective-permute-start.6 = (f32[2,40,1024]{2,1,0:T(8,128)S(1)}, f32[2,40,1024]{2,1,0:T(8,128)S(1)}, u32[]{:S(2)}, u32[]{:S(2)}) collective-permute-start(f32[2,40,1024]{2,1,0:T(8,128)S(1)} %get-tuple-element.45), channel_id=1, source_target_pairs={{0,4},{4,0},{1,5},{5,1},{2,6},{6,2},{3,7},{7,3},{8,12},{12,8},{9,1... | collective-permute-start | bytes 983048 | tf_op jit(solution)/shard_map/ppermute | solution.py:494
  38.1 4.5 %collective-permute-done.5.cross_in = f32[2,40,1024]{2,1,0:T(8,128)S(1)} collective-permute-done((f32[2,40,1024]{2,1,0:T(8,128)S(1)}, f32[2,40,1024]{2,1,0:T(8,128)S(1)}, u32[]{:S(2)}, u32[]{:S(2)}) %collective-permute-start.5) | collective-permute-done | bytes 327712 | tf_op jit(solution)/shard_map/ppermute | solution.py:490
  42.6 0.0 collective-permute-done.6.within_in
  42.6 0.9 shard_map.81
  43.5 1.9 %collective-permute-start.7 = (f32[2,40,1024]{2,1,0:T(8,128)S(1)}, f32[2,40,1024]{2,1,0:T(8,128)S(1)}, u32[]{:S(2)}, u32[]{:S(2)}) collective-permute-start(f32[2,40,1024]{2,1,0:T(8,128)S(1)} %get-tuple-element.48), channel_id=1, source_target_pairs={{4,8},{12,16},{20,24},{28,32},{36,40},{44,48},{52,56},{60,64},{68,... | collective-permute-start | bytes 983048 | tf_op jit(solution)/shard_map/ppermute | solution.py:490
  45.4 1.9 %collective-permute-start.8 = (f32[2,40,1024]{2,1,0:T(8,128)S(1)}, f32[2,40,1024]{2,1,0:T(8,128)S(1)}, u32[]{:S(2)}, u32[]{:S(2)}) collective-permute-start(f32[2,40,1024]{2,1,0:T(8,128)S(1)} %get-tuple-element.49), channel_id=1, source_target_pairs={{0,4},{4,0},{1,5},{5,1},{2,6},{6,2},{3,7},{7,3},{8,12},{12,8},{9,1... | collective-permute-start | bytes 983048 | tf_op jit(solution)/shard_map/ppermute | solution.py:494
  47.3 0.1 shard_map.82.sums_1
  47.4 0.1 shard_map.83.sums_2
  47.4 4.4 %collective-permute-done.7.cross_in = f32[2,40,1024]{2,1,0:T(8,128)S(1)} collective-permute-done((f32[2,40,1024]{2,1,0:T(8,128)S(1)}, f32[2,40,1024]{2,1,0:T(8,128)S(1)}, u32[]{:S(2)}, u32[]{:S(2)}) %collective-permute-start.7) | collective-permute-done | bytes 327712 | tf_op jit(solution)/shard_map/ppermute | solution.py:490
  51.9 0.0 collective-permute-done.8.within_in
  51.9 0.4 shard_map.84
  52.3 25.2 %all_to_all.10.x = f32[16,1,128]{2,1,0:T(1,128)S(1)} all-to-all(f32[16,1,128]{2,1,0:T(1,128)S(1)} %get-tuple-element.50), channel_id=1, replica_groups=mesh['win_0'=8,'win_1'=8,'win_2'=2,'tile'=4] {'win_0','win_2'}, dimensions={0} | all-to-all | bytes 16384 | tf_op jit(solution)/shard_map/all_to_all | solution.py:553
  77.6 12.5 %all_to_all.11.parts = f32[32,1,128]{2,1,0:T(1,128)S(1)} all-to-all(f32[32,1,128]{2,1,0:T(1,128)S(1)} %shard_map.85), channel_id=1, replica_groups=mesh['win_0'=8,'win_1'=8,'win_2'=2,'tile'=4] {'win_1','tile'}, dimensions={0} | all-to-all | bytes 32768 | tf_op jit(solution)/shard_map/all_to_all | solution.py:555
  90.1 1.1 %shard_map.86 = (f32[2,32,1024]{2,1,0:T(8,128)}, f32[2,32,1024]{2,1,0:T(8,128)}) custom-call(f32[32,1,128]{2,1,0:T(1,128)S(1)} %all_to_all.11.parts, f32[2,48,1024]{2,1,0:T(8,128)S(1)} %get-tuple-element.34.b_e.x.q0, f32[2,48,1024]{2,1,0:T(8,128)S(1)} %get-tuple-element.41.q1.y.x, f32[2,48,1024]{2,1,0:T(8,128)S(1)} %get-tuple-element.46.y.q2, ...), custom_call_target="tpu_custom_call" | custom-call | tf_op jit(solution)/shard_map/pallas_call | solution.py:556
  (1 shorter events, 0.0 us)
Async XLA Ops:
  2.5 7.2 %collective-permute-start = (f32[64,1024]{1,0:T(8,128)S(1)}, f32[64,1024]{1,0:T(8,128)S(1)}, u32[]{:S(2)}, u32[]{:S(2)}) collective-permute-start(f32[64,1024]{1,0:T(8,128)S(1)} %get-tuple-element.28), channel_id=1, source_target_pairs={{0,1},{1,2},{2,3},{4,5},{5,6},{6,7},{8,9},{9,10},{10,11},{12,13},{... | collective-permute-start | bytes 786440 | tf_op jit(solution)/shard_map/ppermute | solution.py:478
  6.4 7.1 %collective-permute-start.1 = (f32[64,1024]{1,0:T(8,128)S(1)}, f32[64,1024]{1,0:T(8,128)S(1)}, u32[]{:S(2)}, u32[]{:S(2)}) collective-permute-start(f32[64,1024]{1,0:T(8,128)S(1)} %get-tuple-element.29), channel_id=1, source_target_pairs={{1,0},{2,1},{3,2},{5,4},{6,5},{7,6},{9,8},{10,9},{11,10},{13,12},{... | collective-permute-start | bytes 786440 | tf_op jit(solution)/shard_map/ppermute | solution.py:478
  13.9 19.5 %collective-permute-start.4 = (f32[4,48,1024]{2,1,0:T(8,128)S(1)}, f32[4,48,1024]{2,1,0:T(8,128)S(1)}, u32[]{:S(2)}, u32[]{:S(2)}) collective-permute-start(f32[4,48,1024]{2,1,0:T(8,128)S(1)} %get-tuple-element.40), channel_id=1, source_target_pairs={{0,4},{4,0},{1,5},{5,1},{2,6},{6,2},{3,7},{7,3},{8,12},{12,8},{9,1... | collective-permute-start | bytes 2359304 | tf_op jit(solution)/shard_map/ppermute | solution.py:494
  21.2 12.3 %collective-permute-start.2 = (f32[4,32,1024]{2,1,0:T(8,128)S(1)}, f32[4,32,1024]{2,1,0:T(8,128)S(1)}, u32[]{:S(2)}, u32[]{:S(2)}) collective-permute-start(f32[4,32,1024]{2,1,0:T(8,128)S(1)} %shard_map.79), channel_id=1, source_target_pairs={{4,8},{12,16},{20,24},{28,32},{36,40},{44,48},{52,56},{60,64},{68,... | collective-permute-start | bytes 1572872 | tf_op jit(solution)/shard_map/ppermute | solution.py:490
  23.1 10.3 %collective-permute-start.3 = (f32[40,1024]{1,0:T(8,128)S(1)}, f32[40,1024]{1,0:T(8,128)S(1)}, u32[]{:S(2)}, u32[]{:S(2)}) collective-permute-start(f32[40,1024]{1,0:T(8,128)S(1)} %get-tuple-element.39), channel_id=1, source_target_pairs={{4,8},{12,16},{20,24},{28,32},{36,40},{44,48},{52,56},{60,64},{68,... | collective-permute-start | bytes 491528 | tf_op jit(solution)/shard_map/ppermute | solution.py:490
  34.2 8.4 %collective-permute-start.5 = (f32[2,40,1024]{2,1,0:T(8,128)S(1)}, f32[2,40,1024]{2,1,0:T(8,128)S(1)}, u32[]{:S(2)}, u32[]{:S(2)}) collective-permute-start(f32[2,40,1024]{2,1,0:T(8,128)S(1)} %get-tuple-element.44), channel_id=1, source_target_pairs={{4,8},{12,16},{20,24},{28,32},{36,40},{44,48},{52,56},{60,64},{68,... | collective-permute-start | bytes 983048 | tf_op jit(solution)/shard_map/ppermute | solution.py:490
  36.1 6.5 %collective-permute-start.6 = (f32[2,40,1024]{2,1,0:T(8,128)S(1)}, f32[2,40,1024]{2,1,0:T(8,128)S(1)}, u32[]{:S(2)}, u32[]{:S(2)}) collective-permute-start(f32[2,40,1024]{2,1,0:T(8,128)S(1)} %get-tuple-element.45), channel_id=1, source_target_pairs={{0,4},{4,0},{1,5},{5,1},{2,6},{6,2},{3,7},{7,3},{8,12},{12,8},{9,1... | collective-permute-start | bytes 983048 | tf_op jit(solution)/shard_map/ppermute | solution.py:494
  43.5 8.4 %collective-permute-start.7 = (f32[2,40,1024]{2,1,0:T(8,128)S(1)}, f32[2,40,1024]{2,1,0:T(8,128)S(1)}, u32[]{:S(2)}, u32[]{:S(2)}) collective-permute-start(f32[2,40,1024]{2,1,0:T(8,128)S(1)} %get-tuple-element.48), channel_id=1, source_target_pairs={{4,8},{12,16},{20,24},{28,32},{36,40},{44,48},{52,56},{60,64},{68,... | collective-permute-start | bytes 983048 | tf_op jit(solution)/shard_map/ppermute | solution.py:490
  45.4 6.5 %collective-permute-start.8 = (f32[2,40,1024]{2,1,0:T(8,128)S(1)}, f32[2,40,1024]{2,1,0:T(8,128)S(1)}, u32[]{:S(2)}, u32[]{:S(2)}) collective-permute-start(f32[2,40,1024]{2,1,0:T(8,128)S(1)} %get-tuple-element.49), channel_id=1, source_target_pairs={{0,4},{4,0},{1,5},{5,1},{2,6},{6,2},{3,7},{7,3},{8,12},{12,8},{9,1... | collective-permute-start | bytes 983048 | tf_op jit(solution)/shard_map/ppermute | solution.py:494
where the time goes:
time: 91.7 us; the launch traced here: 91.1 us
  blocking collectives  37.8 us (41%)
  starting transfers between devices  25.7 us (28%)
  waiting for transfers between devices  21.2 us (23%)
  Pallas kernels  5.66 us (6%)
    all_to_all x1, blocking collectives, solve(): moments = lax.all_to_all(moments, near, 0, 0, tiled=True)  25.2 us
    ppermute x4, waiting for transfers between devices, over_chips(): return lax.ppermute(x, WIN, pairs + [(b, a) for a, b in pairs])  15.6 us
    all_to_all x1, blocking collectives, solve(): moments = lax.all_to_all(moments, far, 0, 0, tiled=True)  12.5 us
    ppermute x3, starting transfers between devices, on_chip(): return lax.ppermute(x, 'win_2', [(0, 1), (1, 0)])  11.1 us
    ppermute x4, starting transfers between devices, over_chips(): return lax.ppermute(x, WIN, pairs + [(b, a) for a, b in pairs])  9.4 us
    ppermute x2, waiting for transfers between devices, shifted(): lax.ppermute(x, axis, [(i, i + by) for i in range(count) if 0 <= i + by <...  5.58 us
    ppermute x2, starting transfers between devices, shifted(): lax.ppermute(x, axis, [(i, i + by) for i in range(count) if 0 <= i + by <...  5.24 us
  transfers between devices with their start and end apart: 9, of which 5 were waited for; matrix products, arithmetic and copies ran while one was open for 0% of the time, Pallas kernels for 0%

commit v1 on v0

--- a/solution.py
+++ b/solution.py
@@ -194,6 +194,15 @@
     return lax.axis_index("win_2") == 1
 
 
+def by_core(on_one, on_zero):
+    pl.when(core_is_one())(on_one)
+    pl.when(jnp.logical_not(core_is_one()))(on_zero)
+
+
+def tile_of(ref):
+    return lambda lev, tile: ref[lev, 8 * tile : 8 * tile + 8, :]
+
+
 def ghosts_kernel(from_north, from_south, b_in, c_in, w_in, d_in, b_e, c_e, w_e, d_e, p, cross, within):
     levels, total, width = b_e.shape
     rows = total - 2 * G
@@ -230,14 +239,6 @@
                 cross[high : high + 5, :] = field[lev, G + rows : G + rows + 5, :]
             within[lev] = p[lev]
             within[levels + lev] = p[lev]
-
-
-def unposted(ref, lev, tile, tiles):
-    if tile == 0:
-        return pltpu.roll(ref[lev, 0:8, :], 4, axis=0)
-    if tile == tiles - 1:
-        return pltpu.roll(ref[lev, 8 * tile - 8 : 8 * tile, :], 4, axis=0)
-    return ref[lev, 8 * tile - 4 : 8 * tile + 4, :]
 
 
 def second_half(q, c, w, d, p, v_next, w_next, p_prev, out, edge):
@@ -324,9 +325,6 @@
             p_prev[lev, 4:9, :] = cross_in[at : at + 5, :]
             p_prev[lev, G + rows - 1 : G + rows + 4, :] = cross_in[at + 5 : at + 10, :]
 
-    def tile_of(ref):
-        return lambda lev, tile: ref[lev, 8 * tile : 8 * tile + 8, :]
-
     second_half(
         b_e, c, w, d, p0, tile_of(v_next), tile_of(w_next), tile_of(p_prev), q1, edge
     )
@@ -335,79 +333,84 @@
 
 
 def apply_kernel(
-    q1, c, w, d, p1, w_next, cross_in, within_in, q2, p2, cross, within, edge
+    q1, c, w, d, p1, w_next, cross_in, within_in,
+    q2, p2, early, late, within, edge, v_next, p_prev,
 ):
-    _, total, _ = q1.shape
-    tiles = total // 8
-    one = core_is_one()
-
-    def v_next(lev, tile):
-        return jnp.where(
-            one, unposted(cross_in, lev, tile, tiles), unposted(within_in, lev, tile, tiles)
-        )
-
-    def p_prev(lev, tile):
-        return jnp.where(
-            one, unposted(within_in, lev, tile, tiles), unposted(cross_in, lev, tile, tiles)
-        )
-
+    levels, total, width = q1.shape
+    rows = total - 2 * G
+
+    def assemble(state, image):
+        for lev in range(levels):
+            for out, src in ((v_next, state), (p_prev, image)):
+                out[lev, 0:8, :] = jnp.zeros((8, width), F32)
+                out[lev, total - 8 :, :] = jnp.zeros((8, width), F32)
+                out[lev, 4 : total - 4, :] = src[lev]
+
+    by_core(lambda: assemble(cross_in, within_in), lambda: assemble(within_in, cross_in))
     second_half(
-        q1, c, w, d, p1, v_next,
-        lambda lev, tile: w_next[lev, 8 * tile : 8 * tile + 8, :], p_prev, q2, edge,
+        q1, c, w, d, p1, tile_of(v_next), tile_of(w_next), tile_of(p_prev), q2, edge
     )
     propagate(q2, c, p2)
-    send_both(q2, p2, cross, within)
-
-
-def moments_kernel(q2, c, w, d, p2, w_next, cross_in, within_in, sums_1, sums_2, out, q3, edge, v_next, p_prev):
+
+    def send_up():
+        early[...] = p2[1, G : G + rows, :]
+        late[0:rows, :] = p2[0, G : G + rows, :]
+        late[rows:, :] = jnp.zeros((late.shape[0] - rows, width), F32)
+        for lev in range(levels):
+            post(within, q2, lev)
+
+    def send_down():
+        early[...] = q2[0, G : G + rows, :]
+        late[0 : rows + 2, :] = q2[1, G - 1 : G + rows + 1, :]
+        late[rows + 2 : rows + 3, :] = q2[0, G - 1 : G, :]
+        late[rows + 3 : rows + 4, :] = q2[0, G + rows : G + rows + 1, :]
+        late[rows + 4 :, :] = jnp.zeros((late.shape[0] - rows - 4, width), F32)
+        for lev in range(levels):
+            post(within, p2, lev)
+
+    by_core(send_up, send_down)
+
+
+def moments_kernel(q2, w, d, p2, w_next, early_in, within_in, sums_1, sums_2, out, last):
     levels, total, _ = q2.shape
-    tiles = total // 8
-    one = core_is_one()
-    first = jnp.logical_and(
-        lax.axis_index("win_0") + lax.axis_index("win_1") == 0, jnp.logical_not(one)
-    )
-
-    @pl.when(one)
-    def _():
-        v_next[...] = cross_in[...]
-        p_prev[...] = within_in[...]
-
-    @pl.when(jnp.logical_not(one))
-    def _():
-        v_next[...] = within_in[...]
-        p_prev[...] = cross_in[...]
-
-    last = jnp.zeros((8, 128), F32)
-    for lev in range(levels):
-        for tile in range(1, tiles - 1):
-            at = slice(8 * tile, 8 * tile + 8)
-            here, weight = q2[lev, at, :], w[lev, at, :]
-            gap = v_next[lev, 8 * tile - 4 : 8 * tile + 4, :] - p2[lev, at, :]
-            following = w_next[lev, at, :] * gap
-            diagonal = d[lev, at, :] - THETA
-            own = diagonal + jnp.where(first, weight, 0.0)
-            last = last + folded(following * gap + own * here * here)
-            edge[lev, at, :] = c[1, lev, at, :] * following
-            q3[lev, at, :] = (
-                (weight + diagonal) * here
-                - weight * p_prev[lev, 8 * tile - 4 : 8 * tile + 4, :]
-                - c[0, lev, at, :] * following
-                - west(c[2, lev, at, :] * following)
-                - east(c[3, lev, at, :] * following)
+    rows = total - 2 * G
+    opening = lax.axis_index("win_0") + lax.axis_index("win_1") == 0
+
+    def sum_of(term):
+        amount = jnp.zeros((8, 128), F32)
+        for at in range(0, rows, 8):
+            amount = amount + folded(term(at, slice(G + at, G + at + 8)))
+        return amount
+
+    def squared(weight, gap):
+        return weight * gap * gap
+
+    base = jnp.zeros((8, 128), F32)
+    for lev in range(levels):
+        base = base + sum_of(lambda at, own: squared(d[lev, own, :] - THETA, q2[lev, own, :]))
+
+    def on_one():
+        last[...] = base + sum_of(
+            lambda at, own: squared(w_next[0, own, :], early_in[at : at + 8, :] - p2[0, own, :])
+        )
+
+    def on_zero():
+        amount = base + sum_of(
+            lambda at, own: squared(w[1, own, :], q2[1, own, :] - early_in[at : at + 8, :])
+        )
+        for lev in range(levels):
+            amount = amount + sum_of(
+                lambda at, own: squared(
+                    w_next[lev, own, :], within_in[lev, at + 4 : at + 12, :] - p2[lev, own, :]
+                )
             )
-        for row, at in ((G - 1, 3), (total - G, total - G - 4)):
-            following = w_next[lev, row : row + 1, :] * (
-                v_next[lev, at : at + 1, :] - p2[lev, row : row + 1, :]
-            )
-            edge[lev, row : row + 1, :] = c[1, lev, row : row + 1, :] * following
-        for tile in range(1, tiles - 1):
-            at = slice(8 * tile, 8 * tile + 8)
-            q3[lev, at, :] = q3[lev, at, :] - (
-                north_of(edge, lev, tile) + south_of(edge, lev, tile, tiles)
-            )
+        first = sum_of(lambda at, own: squared(w[0, own, :], q2[0, own, :]))
+        last[...] = amount + jnp.where(opening, first, 0.0)
+
+    by_core(on_one, on_zero)
     lane = lax.broadcasted_iota(jnp.int32, (1, 128), 1)
     result = jnp.zeros((1, 128), F32)
-    parts = [sums_1[2], sums_1[0], sums_1[1], sums_2[0], sums_2[1], last]
+    parts = [sums_1[2], sums_1[0], sums_1[1], sums_2[0], sums_2[1], last[...]]
     for i, part in enumerate(parts):
         total_i = jnp.sum(jnp.sum(part, axis=0, keepdims=True), axis=1, keepdims=True)
         result = jnp.where(lane == i, jnp.broadcast_to(total_i, (1, 128)), result)
@@ -415,10 +418,56 @@
         out[i] = result
 
 
-def spread_kernel(x, out):
-    total = summed(x)
+def spread_kernel(
+    x, q2, c, w, d, p2, w_next, early_in, late_in, within_in,
+    out, q3, edge, v_next, p_prev,
+):
+    levels, total, _ = q2.shape
+    rows = total - 2 * G
+    tiles = total // 8
     for i in range(out.shape[0]):
-        out[i] = total
+        out[i] = x[0]
+
+    def on_one():
+        v_next[0, G : G + rows, :] = early_in[...]
+        v_next[0, G - 1 : G, :] = late_in[rows + 2 : rows + 3, :]
+        v_next[0, G + rows : G + rows + 1, :] = late_in[rows + 3 : rows + 4, :]
+        v_next[1, G - 1 : G + rows + 1, :] = late_in[0 : rows + 2, :]
+        for lev in range(levels):
+            p_prev[lev, :, :] = within_in[lev, 4 : 4 + rows, :]
+
+    def on_zero():
+        p_prev[0, :, :] = late_in[0:rows, :]
+        p_prev[1, :, :] = early_in[...]
+        for lev in range(levels):
+            v_next[lev, 4 : total - 4, :] = within_in[lev]
+
+    by_core(on_one, on_zero)
+    for lev in range(levels):
+        for at in (slice(G - 1, G), slice(G + rows, G + rows + 1)):
+            following = w_next[lev, at, :] * (v_next[lev, at, :] - p2[lev, at, :])
+            edge[lev, at, :] = c[1, lev, at, :] * following
+        for tile in range(1, tiles - 1):
+            at, own = slice(8 * tile, 8 * tile + 8), slice(8 * tile - G, 8 * tile - G + 8)
+            weight = w[lev, at, :]
+            following = w_next[lev, at, :] * (v_next[lev, at, :] - p2[lev, at, :])
+            edge[lev, at, :] = c[1, lev, at, :] * following
+            q3[lev, own, :] = (
+                (weight + d[lev, at, :] - THETA) * q2[lev, at, :]
+                - weight * p_prev[lev, own, :]
+                - c[0, lev, at, :] * following
+                - west(c[2, lev, at, :] * following)
+                - east(c[3, lev, at, :] * following)
+            )
+        for tile in range(1, tiles - 1):
+            own = slice(8 * tile - G, 8 * tile - G + 8)
+            q3[lev, own, :] = q3[lev, own, :] - (
+                north_of(edge, lev, tile) + south_of(edge, lev, tile, tiles)
+            )
+
+
+def total_kernel(x, out):
+    out[0] = summed(x)
 
 
 def summed(x):
@@ -468,9 +517,10 @@
     r = [wide(v) for v in r]
     for lev in range(levels):
         for at in range(0, rows, 8):
-            s = [q[lev, G + at : G + at + 8, :] for q in (q0, q1, q2, q3)]
+            s = [q[lev, G + at : G + at + 8, :] for q in (q0, q1, q2)]
+            last = q3[lev, at : at + 8, :]
             solution_field[lev, at : at + 8, :] = x[0] * s[0] + x[1] * s[1] + x[2] * s[2]
-            residual[lev, at : at + 8, :] = r[0] * s[0] + r[1] * s[1] + r[2] * s[2] + r[3] * s[3]
+            residual[lev, at : at + 8, :] = r[0] * s[0] + r[1] * s[1] + r[2] * s[2] + r[3] * last
 
 
 def shifted(x, axis, by):
@@ -538,20 +588,31 @@
     )(b_e, c_e, w_e, d_e, p0, cross_own, cross, within)
     cross, within = exchanged(cross, within)
     (sums_1,) = call(products_kernel, [shape(3, 8, 128)], count=2)(b_e, q1)
-    q2, p2, cross, within = call(
-        apply_kernel, [field, field, message, message], count=8, scratch=(scratch,)
+    q2, p2, early, late, within = call(
+        apply_kernel,
+        [field, field, shape(rows, width), shape(rows + 8, width), message],
+        count=8,
+        scratch=(scratch,) * 3,
     )(q1, c_e, w_e, d_e, p1, w_next, cross, within)
-    cross, within = exchanged(cross, within)
+    early = over_chips(early)
+    within = on_chip(within)
+    late = over_chips(late)
     (sums_2,) = call(products_kernel, [shape(2, 8, 128)], count=2)(q1, q2)
     near, far = ("win_0", "win_2"), ("win_1", "tile")
+    (moments,) = call(
+        moments_kernel,
+        [shape(lax.axis_size(near), 1, 128)],
+        count=9,
+        scratch=(pltpu.VMEM((8, 128), F32),),
+    )(q2, w_e, d_e, p2, w_next, early, within, sums_1, sums_2)
+    moments = lax.all_to_all(moments, near, 0, 0, tiled=True)
+    (moments,) = call(total_kernel, [shape(1, 1, 128)], count=1)(moments)
     moments, q3 = call(
-        moments_kernel,
-        [shape(lax.axis_size(near), 1, 128), field],
+        spread_kernel,
+        [shape(lax.axis_size(far), 1, 128), own],
         count=10,
-        scratch=(scratch,) + (pltpu.VMEM((levels, rows + 8, width), F32),) * 2,
-    )(q2, c_e, w_e, d_e, p2, w_next, cross, within, sums_1, sums_2)
-    moments = lax.all_to_all(moments, near, 0, 0, tiled=True)
-    (moments,) = call(spread_kernel, [shape(lax.axis_size(far), 1, 128)], count=1)(moments)
+        scratch=(scratch, scratch, pltpu.VMEM((levels, rows, width), F32)),
+    )(moments, q2, c_e, w_e, d_e, p2, w_next, early, late, within)
     moments = lax.all_to_all(moments, far, 0, 0, tiled=True)
     solution_field, residual = call(finish_kernel, [own, own], count=5)(moments, b_e, q1, q2, q3)
     return solution_field[None], residual[None]

time: 91.7 us -> 96.2 us (1.049)
  starting transfers between devices: 25.7 us -> 29.4 us
  blocking collectives: 37.8 us -> 40.4 us
  waiting for transfers between devices: 21.2 us -> 19.4 us
    ppermute x4 -> x5, starting transfers between devices: 9.4 us -> 13 us  [over_chips(): return lax.ppermute(x, WIN, pairs + [(b, a) for a, b in pairs])]
    all_to_all x1, blocking collectives: 25.2 us -> 27.9 us  [solve(): moments = lax.all_to_all(moments, near, 0, 0, tiled=True)]
    ppermute x4 -> x5, waiting for transfers between devices: 15.6 us -> 13.8 us  [over_chips(): return lax.ppermute(x, WIN, pairs + [(b, a) for a, b in pairs])]
  transfers between devices with their start and end apart: 9 -> 10, of which waited for: 5 -> 5; matrix products, arithmetic and copies ran while one was open for 0% -> 0% of each run, Pallas kernels for 0% -> 1%
where the time goes in v1:
time: 96.2 us; the launch traced here: 95.6 us
  blocking collectives  40.4 us (42%)
  starting transfers between devices  29.4 us (31%)
  waiting for transfers between devices  19.4 us (20%)
  Pallas kernels  5.62 us (6%)
    all_to_all x1, blocking collectives, solve(): moments = lax.all_to_all(moments, near, 0, 0, tiled=True)  27.9 us
    ppermute x5, waiting for transfers between devices, over_chips(): return lax.ppermute(x, WIN, pairs + [(b, a) for a, b in pairs])  13.8 us
    ppermute x5, starting transfers between devices, over_chips(): return lax.ppermute(x, WIN, pairs + [(b, a) for a, b in pairs])  13 us
    all_to_all x1, blocking collectives, solve(): moments = lax.all_to_all(moments, far, 0, 0, tiled=True)  12.5 us
    ppermute x3, starting transfers between devices, on_chip(): return lax.ppermute(x, 'win_2', [(0, 1), (1, 0)])  11.1 us
    ppermute x2, waiting for transfers between devices, shifted(): lax.ppermute(x, axis, [(i, i + by) for i in range(count) if 0 <= i + by <...  5.58 us
    ppermute x2, starting transfers between devices, shifted(): lax.ppermute(x, axis, [(i, i + by) for i in range(count) if 0 <= i + by <...  5.24 us
  transfers between devices with their start and end apart: 10, of which 5 were waited for; matrix products, arithmetic and copies ran while one was open for 0% of the time, Pallas kernels for 1%

profile of v1, /device:TPU:1, one launch (start us, length us, event | category | flops | bytes accessed | tf_op | source)
XLA Modules:
  0.0 95.6 jit_solution(16701627588755900943)
XLA Ops:
  0.6 1.8 %shard_map.77 = (f32[64,1024]{1,0:T(8,128)S(1)}, f32[64,1024]{1,0:T(8,128)S(1)}, f32[2,48,1024]{2,1,0:T(8,128)S(1)}, f32[4,2,48,1024]{3,2,1,0:T(8,128)S(1)}, f32...) custom-call(f32[2,32,1024]{2,1,0:T(8,128)} %bitcast.8, f32[4,2,32,1024]{3,2,1,0:T(8,128)} %bitcast.7, ...), custom_call_target="tpu_custom_call" | custom-call | tf_op jit(solution)/shard_map/pallas_call | solution.py:559
  2.5 3.9 %collective-permute-start = (f32[64,1024]{1,0:T(8,128)S(1)}, f32[64,1024]{1,0:T(8,128)S(1)}, u32[]{:S(2)}, u32[]{:S(2)}) collective-permute-start(f32[64,1024]{1,0:T(8,128)S(1)} %get-tuple-element.29), channel_id=1, source_target_pairs={{0,1},{1,2},{2,3},{4,5},{5,6},{6,7},{8,9},{9,10},{10,11},{12,13},{... | collective-permute-start | bytes 786440 | tf_op jit(solution)/shard_map/ppermute | solution.py:528
  6.4 1.3 %collective-permute-start.1 = (f32[64,1024]{1,0:T(8,128)S(1)}, f32[64,1024]{1,0:T(8,128)S(1)}, u32[]{:S(2)}, u32[]{:S(2)}) collective-permute-start(f32[64,1024]{1,0:T(8,128)S(1)} %get-tuple-element.30), channel_id=1, source_target_pairs={{1,0},{2,1},{3,2},{5,4},{6,5},{7,6},{9,8},{10,9},{11,10},{13,12},{... | collective-permute-start | bytes 786440 | tf_op jit(solution)/shard_map/ppermute | solution.py:528
  7.7 0.2 shard_map.79
  7.9 1.8 %collective-permute-done.from_north = f32[64,1024]{1,0:T(8,128)S(1)} collective-permute-done((f32[64,1024]{1,0:T(8,128)S(1)}, f32[64,1024]{1,0:T(8,128)S(1)}, u32[]{:S(2)}, u32[]{:S(2)}) %collective-permute-start) | collective-permute-done | bytes 262176 | tf_op jit(solution)/shard_map/ppermute | solution.py:528
  9.7 3.8 %collective-permute-done.1.from_south = f32[64,1024]{1,0:T(8,128)S(1)} collective-permute-done((f32[64,1024]{1,0:T(8,128)S(1)}, f32[64,1024]{1,0:T(8,128)S(1)}, u32[]{:S(2)}, u32[]{:S(2)}) %collective-permute-start.1) | collective-permute-done | bytes 262176 | tf_op jit(solution)/shard_map/ppermute | solution.py:528
  13.5 0.4 shard_map.78
  13.9 7.2 %collective-permute-start.4 = (f32[4,48,1024]{2,1,0:T(8,128)S(1)}, f32[4,48,1024]{2,1,0:T(8,128)S(1)}, u32[]{:S(2)}, u32[]{:S(2)}) collective-permute-start(f32[4,48,1024]{2,1,0:T(8,128)S(1)} %get-tuple-element.41), channel_id=1, source_target_pairs={{0,4},{4,0},{1,5},{5,1},{2,6},{6,2},{3,7},{7,3},{8,12},{12,8},{9,1... | collective-permute-start | bytes 2359304 | tf_op jit(solution)/shard_map/ppermute | solution.py:544
  21.2 1.9 %collective-permute-start.2 = (f32[4,32,1024]{2,1,0:T(8,128)S(1)}, f32[4,32,1024]{2,1,0:T(8,128)S(1)}, u32[]{:S(2)}, u32[]{:S(2)}) collective-permute-start(f32[4,32,1024]{2,1,0:T(8,128)S(1)} %shard_map.79), channel_id=1, source_target_pairs={{4,8},{12,16},{20,24},{28,32},{36,40},{44,48},{52,56},{60,64},{68,... | collective-permute-start | bytes 1572872 | tf_op jit(solution)/shard_map/ppermute | solution.py:540
  23.1 3.6 %collective-permute-start.3 = (f32[40,1024]{1,0:T(8,128)S(1)}, f32[40,1024]{1,0:T(8,128)S(1)}, u32[]{:S(2)}, u32[]{:S(2)}) collective-permute-start(f32[40,1024]{1,0:T(8,128)S(1)} %get-tuple-element.40), channel_id=1, source_target_pairs={{4,8},{12,16},{20,24},{28,32},{36,40},{44,48},{52,56},{60,64},{68,... | collective-permute-start | bytes 491528 | tf_op jit(solution)/shard_map/ppermute | solution.py:540
  26.8 6.7 %collective-permute-done.3.cross_in = f32[40,1024]{1,0:T(8,128)S(1)} collective-permute-done((f32[40,1024]{1,0:T(8,128)S(1)}, f32[40,1024]{1,0:T(8,128)S(1)}, u32[]{:S(2)}, u32[]{:S(2)}) %collective-permute-start.3) | collective-permute-done | bytes 163872 | tf_op jit(solution)/shard_map/ppermute | solution.py:540
  33.4 0.0 collective-permute-done.2.cross_own
  33.4 0.0 collective-permute-done.4.within_in
  33.5 0.7 shard_map.80
  34.2 1.9 %collective-permute-start.5 = (f32[2,40,1024]{2,1,0:T(8,128)S(1)}, f32[2,40,1024]{2,1,0:T(8,128)S(1)}, u32[]{:S(2)}, u32[]{:S(2)}) collective-permute-start(f32[2,40,1024]{2,1,0:T(8,128)S(1)} %get-tuple-element.45), channel_id=1, source_target_pairs={{4,8},{12,16},{20,24},{28,32},{36,40},{44,48},{52,56},{60,64},{68,... | collective-permute-start | bytes 983048 | tf_op jit(solution)/shard_map/ppermute | solution.py:540
  36.1 1.9 %collective-permute-start.6 = (f32[2,40,1024]{2,1,0:T(8,128)S(1)}, f32[2,40,1024]{2,1,0:T(8,128)S(1)}, u32[]{:S(2)}, u32[]{:S(2)}) collective-permute-start(f32[2,40,1024]{2,1,0:T(8,128)S(1)} %get-tuple-element.46), channel_id=1, source_target_pairs={{0,4},{4,0},{1,5},{5,1},{2,6},{6,2},{3,7},{7,3},{8,12},{12,8},{9,1... | collective-permute-start | bytes 983048 | tf_op jit(solution)/shard_map/ppermute | solution.py:544
  38.1 4.5 %collective-permute-done.5.cross_in = f32[2,40,1024]{2,1,0:T(8,128)S(1)} collective-permute-done((f32[2,40,1024]{2,1,0:T(8,128)S(1)}, f32[2,40,1024]{2,1,0:T(8,128)S(1)}, u32[]{:S(2)}, u32[]{:S(2)}) %collective-permute-start.5) | collective-permute-done | bytes 327712 | tf_op jit(solution)/shard_map/ppermute | solution.py:540
  42.6 0.0 collective-permute-done.6.within_in
  42.6 0.8 shard_map.81
  43.4 1.9 %collective-permute-start.8 = (f32[2,40,1024]{2,1,0:T(8,128)S(1)}, f32[2,40,1024]{2,1,0:T(8,128)S(1)}, u32[]{:S(2)}, u32[]{:S(2)}) collective-permute-start(f32[2,40,1024]{2,1,0:T(8,128)S(1)} %get-tuple-element.50), channel_id=1, source_target_pairs={{0,4},{4,0},{1,5},{5,1},{2,6},{6,2},{3,7},{7,3},{8,12},{12,8},{9,1... | collective-permute-start | bytes 983048 | tf_op jit(solution)/shard_map/ppermute | solution.py:544
  45.3 2.0 %collective-permute-start.9 = (f32[40,1024]{1,0:T(8,128)S(1)}, f32[40,1024]{1,0:T(8,128)S(1)}, u32[]{:S(2)}, u32[]{:S(2)}) collective-permute-start(f32[40,1024]{1,0:T(8,128)S(1)} %get-tuple-element.51), channel_id=1, source_target_pairs={{4,8},{12,16},{20,24},{28,32},{36,40},{44,48},{52,56},{60,64},{68,... | collective-permute-start | bytes 491528 | tf_op jit(solution)/shard_map/ppermute | solution.py:540
  47.3 3.5 %collective-permute-start.7 = (f32[32,1024]{1,0:T(8,128)S(1)}, f32[32,1024]{1,0:T(8,128)S(1)}, u32[]{:S(2)}, u32[]{:S(2)}) collective-permute-start(f32[32,1024]{1,0:T(8,128)S(1)} %get-tuple-element.49), channel_id=1, source_target_pairs={{4,8},{12,16},{20,24},{28,32},{36,40},{44,48},{52,56},{60,64},{68,... | collective-permute-start | bytes 393224 | tf_op jit(solution)/shard_map/ppermute | solution.py:540
  50.9 0.1 shard_map.82.sums_1
  50.9 0.1 shard_map.83.sums_2
  51.0 2.6 %collective-permute-done.7.early_in = f32[32,1024]{1,0:T(8,128)S(1)} collective-permute-done((f32[32,1024]{1,0:T(8,128)S(1)}, f32[32,1024]{1,0:T(8,128)S(1)}, u32[]{:S(2)}, u32[]{:S(2)}) %collective-permute-start.7) | collective-permute-done | bytes 131104 | tf_op jit(solution)/shard_map/ppermute | solution.py:540
  53.6 0.0 collective-permute-done.8.within_in
  53.6 0.2 shard_map.84
  53.8 27.9 %all_to_all.10.x = f32[16,1,128]{2,1,0:T(1,128)S(1)} all-to-all(f32[16,1,128]{2,1,0:T(1,128)S(1)} %shard_map.84), channel_id=1, replica_groups=mesh['win_0'=8,'win_1'=8,'win_2'=2,'tile'=4] {'win_0','win_2'}, dimensions={0} | all-to-all | bytes 16384 | tf_op jit(solution)/shard_map/all_to_all | solution.py:608
  81.7 0.0 collective-permute-done.9.late_in
  81.7 0.3 shard_map.86
  82.1 12.5 %all_to_all.11.parts = f32[32,1,128]{2,1,0:T(1,128)S(1)} all-to-all(f32[32,1,128]{2,1,0:T(1,128)S(1)} %get-tuple-element.52), channel_id=1, replica_groups=mesh['win_0'=8,'win_1'=8,'win_2'=2,'tile'=4] {'win_1','tile'}, dimensions={0} | all-to-all | bytes 32768 | tf_op jit(solution)/shard_map/all_to_all | solution.py:616
  94.6 1.1 %shard_map.87 = (f32[2,32,1024]{2,1,0:T(8,128)}, f32[2,32,1024]{2,1,0:T(8,128)}) custom-call(f32[32,1,128]{2,1,0:T(1,128)S(1)} %all_to_all.11.parts, f32[2,48,1024]{2,1,0:T(8,128)S(1)} %get-tuple-element.35.b_e.x.q0, f32[2,48,1024]{2,1,0:T(8,128)S(1)} %get-tuple-element.42.q1.y.x, f32[2,48,1024]{2,1,0:T(8,128)S(1)} %get-tuple-element.47.y.q2, ...), custom_call_target="tpu_custom_call" | custom-call | tf_op jit(solution)/shard_map/pallas_call | solution.py:617
  (1 shorter events, 0.0 us)
Async XLA Ops:
  2.5 7.2 %collective-permute-start = (f32[64,1024]{1,0:T(8,128)S(1)}, f32[64,1024]{1,0:T(8,128)S(1)}, u32[]{:S(2)}, u32[]{:S(2)}) collective-permute-start(f32[64,1024]{1,0:T(8,128)S(1)} %get-tuple-element.29), channel_id=1, source_target_pairs={{0,1},{1,2},{2,3},{4,5},{5,6},{6,7},{8,9},{9,10},{10,11},{12,13},{... | collective-permute-start | bytes 786440 | tf_op jit(solution)/shard_map/ppermute | solution.py:528
  6.4 7.1 %collective-permute-start.1 = (f32[64,1024]{1,0:T(8,128)S(1)}, f32[64,1024]{1,0:T(8,128)S(1)}, u32[]{:S(2)}, u32[]{:S(2)}) collective-permute-start(f32[64,1024]{1,0:T(8,128)S(1)} %get-tuple-element.30), channel_id=1, source_target_pairs={{1,0},{2,1},{3,2},{5,4},{6,5},{7,6},{9,8},{10,9},{11,10},{13,12},{... | collective-permute-start | bytes 786440 | tf_op jit(solution)/shard_map/ppermute | solution.py:528
  13.9 19.5 %collective-permute-start.4 = (f32[4,48,1024]{2,1,0:T(8,128)S(1)}, f32[4,48,1024]{2,1,0:T(8,128)S(1)}, u32[]{:S(2)}, u32[]{:S(2)}) collective-permute-start(f32[4,48,1024]{2,1,0:T(8,128)S(1)} %get-tuple-element.41), channel_id=1, source_target_pairs={{0,4},{4,0},{1,5},{5,1},{2,6},{6,2},{3,7},{7,3},{8,12},{12,8},{9,1... | collective-permute-start | bytes 2359304 | tf_op jit(solution)/shard_map/ppermute | solution.py:544
  21.2 12.3 %collective-permute-start.2 = (f32[4,32,1024]{2,1,0:T(8,128)S(1)}, f32[4,32,1024]{2,1,0:T(8,128)S(1)}, u32[]{:S(2)}, u32[]{:S(2)}) collective-permute-start(f32[4,32,1024]{2,1,0:T(8,128)S(1)} %shard_map.79), channel_id=1, source_target_pairs={{4,8},{12,16},{20,24},{28,32},{36,40},{44,48},{52,56},{60,64},{68,... | collective-permute-start | bytes 1572872 | tf_op jit(solution)/shard_map/ppermute | solution.py:540
  23.1 10.3 %collective-permute-start.3 = (f32[40,1024]{1,0:T(8,128)S(1)}, f32[40,1024]{1,0:T(8,128)S(1)}, u32[]{:S(2)}, u32[]{:S(2)}) collective-permute-start(f32[40,1024]{1,0:T(8,128)S(1)} %get-tuple-element.40), channel_id=1, source_target_pairs={{4,8},{12,16},{20,24},{28,32},{36,40},{44,48},{52,56},{60,64},{68,... | collective-permute-start | bytes 491528 | tf_op jit(solution)/shard_map/ppermute | solution.py:540
  34.2 8.4 %collective-permute-start.5 = (f32[2,40,1024]{2,1,0:T(8,128)S(1)}, f32[2,40,1024]{2,1,0:T(8,128)S(1)}, u32[]{:S(2)}, u32[]{:S(2)}) collective-permute-start(f32[2,40,1024]{2,1,0:T(8,128)S(1)} %get-tuple-element.45), channel_id=1, source_target_pairs={{4,8},{12,16},{20,24},{28,32},{36,40},{44,48},{52,56},{60,64},{68,... | collective-permute-start | bytes 983048 | tf_op jit(solution)/shard_map/ppermute | solution.py:540
  36.1 6.5 %collective-permute-start.6 = (f32[2,40,1024]{2,1,0:T(8,128)S(1)}, f32[2,40,1024]{2,1,0:T(8,128)S(1)}, u32[]{:S(2)}, u32[]{:S(2)}) collective-permute-start(f32[2,40,1024]{2,1,0:T(8,128)S(1)} %get-tuple-element.46), channel_id=1, source_target_pairs={{0,4},{4,0},{1,5},{5,1},{2,6},{6,2},{3,7},{7,3},{8,12},{12,8},{9,1... | collective-permute-start | bytes 983048 | tf_op jit(solution)/shard_map/ppermute | solution.py:544
  43.4 10.3 %collective-permute-start.8 = (f32[2,40,1024]{2,1,0:T(8,128)S(1)}, f32[2,40,1024]{2,1,0:T(8,128)S(1)}, u32[]{:S(2)}, u32[]{:S(2)}) collective-permute-start(f32[2,40,1024]{2,1,0:T(8,128)S(1)} %get-tuple-element.50), channel_id=1, source_target_pairs={{0,4},{4,0},{1,5},{5,1},{2,6},{6,2},{3,7},{7,3},{8,12},{12,8},{9,1... | collective-permute-start | bytes 983048 | tf_op jit(solution)/shard_map/ppermute | solution.py:544
  45.3 36.4 %collective-permute-start.9 = (f32[40,1024]{1,0:T(8,128)S(1)}, f32[40,1024]{1,0:T(8,128)S(1)}, u32[]{:S(2)}, u32[]{:S(2)}) collective-permute-start(f32[40,1024]{1,0:T(8,128)S(1)} %get-tuple-element.51), channel_id=1, source_target_pairs={{4,8},{12,16},{20,24},{28,32},{36,40},{44,48},{52,56},{60,64},{68,... | collective-permute-start | bytes 491528 | tf_op jit(solution)/shard_map/ppermute | solution.py:540
  47.3 6.3 %collective-permute-start.7 = (f32[32,1024]{1,0:T(8,128)S(1)}, f32[32,1024]{1,0:T(8,128)S(1)}, u32[]{:S(2)}, u32[]{:S(2)}) collective-permute-start(f32[32,1024]{1,0:T(8,128)S(1)} %get-tuple-element.49), channel_id=1, source_target_pairs={{4,8},{12,16},{20,24},{28,32},{36,40},{44,48},{52,56},{60,64},{68,... | collective-permute-start | bytes 393224 | tf_op jit(solution)/shard_map/ppermute | solution.py:540
